TPU v7x, 32 devices: a whole 2x2x4 slice. The times are simulated.
32 devices in a mesh: groups: 2 (over x), gx: 8 (over z, y), gy: 2 (over core).
Axes of the slice: x: 2, y: 2, z: 4, core: 2. Of those that a mesh axis runs over, the one named last changes fastest.
Arguments:
- source: float32 [2, 3, 2, 32, 64, 256], P('groups', None, None, 'gx', 'gy'), parts along dimension 0, may hold values from -12 to 12
- permittivity: float32 [6, 32, 64, 256], P('groups', 'gx', 'gy'), parts along dimension 0, may hold values from 1 to 12
- frequency: float32 [1], replicated, may hold values from 0.25 to 0.6
Outputs:
- solution: float32 [2, 3, 2, 32, 64, 256], P('groups', None, None, 'gx', 'gy'), parts along dimension 0
- residual: float32 [2, 3, 2, 32, 64, 256], P('groups', None, None, 'gx', 'gy'), parts along dimension 0
There are 2 independent parts, one for each index of `groups`. A program takes and returns all parts, laid end to end along the dimension named above; an argument that names none is the same for every part. Nothing has to cross between parts.
All inputs are finite; a program needn't handle non-finite values.
Results may differ from a plain program's by a relative error of at most 0.0003.
Values sent between devices are 32-bit elements; how exact they have to be, the bound alone decides.
A program may use at most 64 MiB of HBM per device.

v0:
```python
import jax
import jax.numpy as jnp
from jax import lax
from jax.sharding import PartitionSpec as P

NZ = 256
PML = 8
ITERS = 3
pml_strength = 2.0


def shifted(array, axis, by):
    devices = lax.axis_size(axis)
    pairs = [(i, i + by) for i in range(devices) if 0 <= i + by < devices]
    return lax.ppermute(array, axis, pairs)


def stretch(points, length, frequency):
    inside = jnp.maximum(jnp.maximum(PML - points, points - (length - PML)), 0.0) / PML
    damping = pml_strength * inside**3 / frequency[:, None]
    factor = 1.0 / (1.0 + damping * damping)
    return jnp.stack([factor, -damping * factor], axis=1)


def orient(coefficient, dimension):
    target = [coefficient.shape[0], 2, 1, 1, 1]
    target[dimension] = coefficient.shape[2]
    return coefficient.reshape(target)


def times_coef(values, coefficient):
    real_part = values[:, 0] * coefficient[:, 0] - values[:, 1] * coefficient[:, 1]
    imag_part = values[:, 0] * coefficient[:, 1] + values[:, 1] * coefficient[:, 0]
    return jnp.stack([real_part, imag_part], axis=1)


def curl_forward(extended, front_x, front_y, front_z):
    centre = extended[:, :, :, :-1, :-1]

    def step_x(component):
        return extended[:, component, :, 1:, :-1] - centre[:, component]

    def step_y(component):
        return extended[:, component, :, :-1, 1:] - centre[:, component]

    def step_z(component):
        cells = centre[:, component]
        above = jnp.concatenate([cells[..., 1:], jnp.zeros_like(cells[..., :1])], axis=-1)
        return above - cells

    curl_x = times_coef(step_y(2), front_y) - times_coef(step_z(1), front_z)
    curl_y = times_coef(step_z(0), front_z) - times_coef(step_x(2), front_x)
    curl_z = times_coef(step_x(1), front_x) - times_coef(step_y(0), front_y)
    return jnp.stack([curl_x, curl_y, curl_z], axis=1)


def curl_backward(padded, back_x, back_y, back_z):
    centre = padded[:, :, :, 1:, 1:]

    def step_x(component):
        return centre[:, component] - padded[:, component, :, :-1, 1:]

    def step_y(component):
        return centre[:, component] - padded[:, component, :, 1:, :-1]

    def step_z(component):
        cells = centre[:, component]
        below = jnp.concatenate([jnp.zeros_like(cells[..., :1]), cells[..., :-1]], axis=-1)
        return cells - below

    out_x = times_coef(step_y(2), back_y) - times_coef(step_z(1), back_z)
    out_y = times_coef(step_z(0), back_z) - times_coef(step_x(2), back_x)
    out_z = times_coef(step_x(1), back_x) - times_coef(step_y(0), back_y)
    return jnp.stack([out_x, out_y, out_z], axis=1)


def scaled(values, number):
    real_scale = number[0].reshape(-1, 1, 1, 1, 1)
    imag_scale = number[1].reshape(-1, 1, 1, 1, 1)
    real_part = values[:, :, 0] * real_scale - values[:, :, 1] * imag_scale
    imag_part = values[:, :, 0] * imag_scale + values[:, :, 1] * real_scale
    return jnp.stack([real_part, imag_part], axis=2)


def product(left, right):
    real_part = jnp.sum(
        left[:, :, 0] * right[:, :, 0] + left[:, :, 1] * right[:, :, 1], axis=(1, 2, 3, 4)
    )
    imag_part = jnp.sum(
        left[:, :, 0] * right[:, :, 1] - left[:, :, 1] * right[:, :, 0], axis=(1, 2, 3, 4)
    )
    return jnp.stack([real_part, imag_part])


def complex_times(first, other):
    return jnp.stack(
        [first[0] * other[0] - first[1] * other[1], first[0] * other[1] + first[1] * other[0]]
    )


def complex_ratio(first, other):
    modulus = other[0] * other[0] + other[1] * other[1]
    return (
        jnp.stack(
            [first[0] * other[0] + first[1] * other[1], first[1] * other[0] - first[0] * other[1]]
        )
        / modulus
    )


def grid_points(start, first, count):
    return (start + jnp.arange(first, count, dtype=jnp.int32)).astype(jnp.float32)


def body(source, permittivity, frequency):
    cells_x = source.shape[3]
    cells_y = source.shape[4]
    total_x = cells_x * lax.axis_size("gx")
    total_y = cells_y * lax.axis_size("gy")
    index_x = lax.axis_index("gx")
    index_y = lax.axis_index("gy")
    margin = 0
    front_x = orient(
        stretch(grid_points(index_x * cells_x, -margin, cells_x) + 0.5, total_x, frequency), 2
    )
    front_y = orient(
        stretch(grid_points(index_y * cells_y, -margin, cells_y) + 0.5, total_y, frequency), 3
    )
    back_x = orient(stretch(grid_points(index_x * cells_x, 0, cells_x), total_x, frequency), 2)
    back_y = orient(stretch(grid_points(index_y * cells_y, 0, cells_y), total_y, frequency), 3)
    z_points = grid_points(0, 0, NZ)
    front_z = orient(stretch(z_points + 0.5, NZ, frequency), 4)
    back_z = orient(stretch(z_points, NZ, frequency), 4)
    material = (frequency * frequency).reshape(-1, 1, 1, 1, 1, 1) * permittivity[None, :, None]

    def operate(values):
        above_x = shifted(values[:, :, :, :1], "gx", -1)
        above_y = shifted(values[:, :, :, :, :1], "gy", -1)
        extended = jnp.concatenate([values, above_x], axis=3)
        side_cells = jnp.concatenate([above_y, jnp.zeros_like(above_y[:, :, :, :1])], axis=3)
        extended = jnp.concatenate([extended, side_cells], axis=4)
        rotated = curl_forward(extended, front_x, front_y, front_z)
        below_x = shifted(rotated[:, :, :, -1:], "gx", 1)
        below_y = shifted(rotated[:, :, :, :, -1:], "gy", 1)
        padded = jnp.concatenate([below_x, rotated], axis=3)
        side_cells = jnp.concatenate([jnp.zeros_like(below_y[:, :, :, :1]), below_y], axis=3)
        padded = jnp.concatenate([side_cells, padded], axis=4)
        applied = curl_backward(padded, back_x, back_y, back_z)
        return applied - material * values

    solution = jnp.zeros_like(source)
    residual = source
    direction = source
    shadow_dot = lax.psum(product(source, residual), ("gx", "gy"))
    for iteration in range(ITERS):
        applied = operate(direction)
        step_size = complex_ratio(shadow_dot, lax.psum(product(source, applied), ("gx", "gy")))
        middle = residual - scaled(applied, step_size)
        second = operate(middle)
        sums_triple = lax.psum(
            (product(second, middle), product(second, second), product(source, second)),
            ("gx", "gy"),
        )
        weight = complex_ratio(sums_triple[0], sums_triple[1])
        solution = solution + scaled(direction, step_size) + scaled(middle, weight)
        residual = middle - scaled(second, weight)
        if iteration + 1 < ITERS:
            shadow_next = -complex_times(weight, sums_triple[2])
            momentum = complex_times(
                complex_ratio(shadow_next, shadow_dot), complex_ratio(step_size, weight)
            )
            direction = residual + scaled(direction - scaled(applied, weight), momentum)
            shadow_dot = shadow_next
    return (solution, residual)


def solution(mesh):
    placed = (P("groups", None, None, "gx", "gy", None), P("groups", "gx", "gy", None), P())
    return jax.shard_map(
        body,
        mesh=mesh,
        in_specs=placed,
        out_specs=(
            P("groups", None, None, "gx", "gy", None),
            P("groups", None, None, "gx", "gy", None),
        ),
        check_vma=False,
    )
```

profile of v0, /device:TPU:0, one launch (start us, length us, event | category | flops | bytes accessed | tf_op | source)
XLA Modules:
  0.0 469.3 jit_solution(13969787863053648633)
XLA Ops:
  1.6 1.3 collective-permute-start.1
  3.9 1.3 collective-permute-start
  7.5 6.7 %collective-permute-done = f32[1,3,2,1,32,256]{5,4,3,2,1,0:T(8,128)S(1)} collective-permute-done((f32[1,3,2,1,32,256]{5,4,3,2,1,0:T(8,128)S(1)}, f32[1,3,2,1,32,256]{5,4,3,2,1,0:T(8,128)S(1)}, u32[]{:S(2)}, u32[]{:S(2)}) %collective-permute-start) | collective-permute-done | bytes 196640 | tf_op jit(solution)/shard_map/ppermute | solution.py:15
  15.4 2.2 collective-permute-start.2
  17.5 5.0 %collective-permute-start.3 = (f32[1,3,2,1,32,256]{5,4,3,2,1,0:T(8,128)S(1)}, f32[1,3,2,1,32,256]{5,4,3,2,1,0:T(8,128)S(1)}, u32[]{:S(2)}, u32[]{:S(2)}) collective-permute-start(f32[1,3,2,1,32,256]{5,4,3,2,1,0:T(8,128)S(1)} %pad_maximum_fusion.33), channel_id=1, source_target_pairs={{0,2},{2,4},{4,6},{6,8},{8,10},{10,12},{12,14},{1,3},{3,5},{5,7},{... | collective-permute-start | bytes 589832 | tf_op jit(solution)/shard_map/ppermute | solution.py:15
  22.5 3.6 collective-permute-done.3
  29.7 1.4 pad_maximum_fusion.41
  31.1 31.3 %all-reduce.39 = (f32[2,1]{1,0:T(2,128)S(1)}, f32[2,1]{1,0:T(2,128)S(1)}) all-reduce(f32[2,1]{1,0:T(2,128)S(1)} %pad_maximum_fusion.41, f32[2,1]{1,0:T(2,128)S(1)} %pad_maximum_fusion.42), channel_id=1, replica_groups=mesh['groups'=2,'gx'=8,'gy'=2] {'gx','gy'}, use_global_device_ids=true, to_apply=%region_2.0 | all-reduce | flops 4 | bytes 32 | tf_op jit(solution)/shard_map/psum | solution.py:154
  71.5 1.3 multiply_subtract_fusion.14
  73.0 1.3 collective-permute-start.4
  74.3 1.3 collective-permute-start.5
  75.6 1.8 collective-permute-done.5
  77.4 3.2 collective-permute-done.4
  81.7 1.5 collective-permute-start.7
  83.2 1.7 collective-permute-start.6
  91.1 1.3 pad_maximum_fusion.45
  94.9 29.5 %all-reduce.38 = (f32[2,1]{1,0:T(2,128)S(1)}, f32[2,1]{1,0:T(2,128)S(1)}, f32[2,1]{1,0:T(2,128)S(1)}) all-reduce(f32[2,1]{1,0:T(2,128)S(1)} %pad_maximum_fusion.43, f32[2,1]{1,0:T(2,128)S(1)} %pad_maximum_fusion.44, f32[2,1]{1,0:T(2,128)S(1)} %pad_maximum_fusion.45), channel_id=1, replica_groups=mesh['groups'=2,'gx'=8,'gy'=2] {'gx','gy'}, use_global_device_ids=true, to_apply=%region_8.0 | all-reduce | flops 6 | bytes 48 | tf_op jit(solution)/shard_map/psum | solution.py:160
  141.5 2.5 multiply_subtract_fusion.11
  144.0 1.4 multiply_subtract_fusion.12
  163.9 1.3 collective-permute-start.8
  165.2 1.3 collective-permute-start.9
  166.5 1.8 collective-permute-done.9
  168.3 4.2 collective-permute-done.8
  173.6 1.5 collective-permute-start.11
  182.1 1.3 pad_maximum_fusion.46
  183.4 30.3 %psum.89 = f32[2,1]{1,0:T(2,128)S(1)} all-reduce(f32[2,1]{1,0:T(2,128)S(1)} %pad_maximum_fusion.46), channel_id=1, replica_groups=mesh['groups'=2,'gx'=8,'gy'=2] {'gx','gy'}, use_global_device_ids=true, to_apply=%region_17.0 | all-reduce | flops 2 | bytes 16 | tf_op jit(solution)/shard_map/psum | solution.py:157
  222.7 2.5 multiply_subtract_fusion.8
  225.6 1.3 collective-permute-start.12
  226.9 1.5 collective-permute-start.13
  228.4 1.6 collective-permute-done.13
  230.0 3.4 collective-permute-done.12
  235.0 1.5 collective-permute-start.15
  236.5 1.5 collective-permute-start.14
  245.7 1.8 pad_maximum_fusion.49
  247.5 1.9 pad_maximum_fusion.48
  249.4 1.9 pad_maximum_fusion.47
  251.3 30.6 %all-reduce.37 = (f32[2,1]{1,0:T(2,128)}, f32[2,1]{1,0:T(2,128)}, f32[2,1]{1,0:T(2,128)}) all-reduce(f32[2,1]{1,0:T(2,128)} %pad_maximum_fusion.47, f32[2,1]{1,0:T(2,128)} %pad_maximum_fusion.48, f32[2,1]{1,0:T(2,128)} %pad_maximum_fusion.49), channel_id=1, replica_groups=mesh['groups'=2,'gx'=8,'gy'=2] {'gx','gy'}, use_global_device_ids=true, to_apply=%region_20.0 | all-reduce | flops 6 | bytes 48 | tf_op jit(solution)/shard_map/psum | solution.py:160
  281.9 1.3 fusion.88
  283.2 1.3 fusion.87
  300.1 2.5 multiply_subtract_fusion.5
  323.3 1.3 collective-permute-start.16
  325.9 1.8 collective-permute-done.17
  327.7 3.7 collective-permute-done.16
  333.0 1.5 collective-permute-start.19
  336.7 1.7 collective-permute-done.19
  342.3 3.0 add_reduce_fusion.2
  345.3 1.8 pad_maximum_fusion.50
  347.1 2.3 multiply_subtract_fusion.13
  349.4 30.0 %psum.93 = f32[2,1]{1,0:T(2,128)S(1)} all-reduce(f32[2,1]{1,0:T(2,128)} %pad_maximum_fusion.50), channel_id=1, replica_groups=mesh['groups'=2,'gx'=8,'gy'=2] {'gx','gy'}, use_global_device_ids=true, to_apply=%region_29.0 | all-reduce | flops 2 | bytes 16 | tf_op jit(solution)/shard_map/psum | solution.py:157
  388.2 2.5 multiply_subtract_fusion.2
  390.7 2.3 maximum_subtract_fusion.11
  393.0 1.3 collective-permute-start.21
  394.3 1.3 collective-permute-start.20
  395.6 2.3 multiply_subtract_fusion.9
  397.9 5.9 %collective-permute-done.20 = f32[1,3,2,1,32,256]{5,4,3,2,1,0:T(8,128)S(1)} collective-permute-done((f32[1,3,2,1,32,256]{5,4,3,2,1,0:T(8,128)S(1)}, f32[1,3,2,1,32,256]{5,4,3,2,1,0:T(8,128)S(1)}, u32[]{:S(2)}, u32[]{:S(2)}) %collective-permute-start.20) | collective-permute-done | bytes 196640 | tf_op jit(solution)/shard_map/ppermute | solution.py:15
  405.4 2.0 collective-permute-start.22
  407.5 1.9 collective-permute-start.23
  409.3 2.2 multiply_subtract_fusion.7
  420.7 2.2 multiply_subtract_fusion.3
  422.9 29.5 %all-reduce.36 = (f32[2,1]{1,0:T(2,128)S(1)}, f32[2,1]{1,0:T(2,128)S(1)}) all-reduce(f32[2,1]{1,0:T(2,128)S(1)} %pad_maximum_fusion.51, f32[2,1]{1,0:T(2,128)S(1)} %pad_maximum_fusion.52), channel_id=1, replica_groups=mesh['groups'=2,'gx'=8,'gy'=2] {'gx','gy'}, use_global_device_ids=true, to_apply=%region_32.0 | all-reduce | flops 4 | bytes 32 | tf_op jit(solution)/shard_map/psum | solution.py:160
  461.4 2.6 multiply_subtract_fusion
  464.1 1.4 multiply_subtract_fusion.1
  465.6 1.5 maximum_subtract_fusion.13
  467.9 1.4 fusion.3
  (423 shorter events, 66.4 us)
Async XLA Ops:
  0.6 6.7 %copy-start.52 = (f32[3,4,32,256]{3,2,1,0:T(8,128)S(1)}, f32[3,4,32,256]{3,2,1,0:T(8,128)}, u32[]{:S(2)}) copy-start(f32[3,4,32,256]{3,2,1,0:T(8,128)} %param.4) | copy-start | bytes 1179652
  1.6 12.5 %collective-permute-start.1 = (f32[1,3,2,4,1,256]{5,4,3,2,1,0:T(1,128)S(1)}, f32[1,3,2,4,1,256]{5,4,3,2,1,0:T(1,128)S(1)}, u32[]{:S(2)}, u32[]{:S(2)}) collective-permute-start(f32[1,3,2,4,1,256]{5,4,3,2,1,0:T(1,128)S(1)} %slice.702), channel_id=1, source_target_pairs={{1,0},{3,2},{5,4},{7,6},{9,8},{11,10},{13,12},{15,14},{17,16},{19,... | collective-permute-start | bytes 73736 | tf_op jit(solution)/shard_map/ppermute | solution.py:15
  3.9 10.2 %collective-permute-start = (f32[1,3,2,1,32,256]{5,4,3,2,1,0:T(8,128)S(1)}, f32[1,3,2,1,32,256]{5,4,3,2,1,0:T(8,128)S(1)}, u32[]{:S(2)}, u32[]{:S(2)}) collective-permute-start(f32[1,3,2,1,32,256]{5,4,3,2,1,0:T(8,128)S(1)} %slice.695), channel_id=1, source_target_pairs={{2,0},{4,2},{6,4},{8,6},{10,8},{12,10},{14,12},{3,1},{5,3},{7,5},{... | collective-permute-start | bytes 589832 | tf_op jit(solution)/shard_map/ppermute | solution.py:15
  7.1 172.1 %copy-start.53 = (f32[4]{0:T(128)}, f32[4]{0:T(128)S(1)}, u32[]{:S(2)}) copy-start(f32[4]{0:T(128)S(1)} %get-tuple-element.424) | copy-start | bytes 52
  7.1 172.1 %copy-start.57 = (f32[4]{0:T(128)}, f32[4]{0:T(128)S(1)}, u32[]{:S(2)}) copy-start(f32[4]{0:T(128)S(1)} %get-tuple-element.425) | copy-start | bytes 52
  7.2 166.2 %copy-start.61 = (f32[4]{0:T(128)}, f32[4]{0:T(128)S(1)}, u32[]{:S(2)}) copy-start(f32[4]{0:T(128)S(1)} %get-tuple-element.432) | copy-start | bytes 52
  7.2 166.2 %copy-start.65 = (f32[4]{0:T(128)}, f32[4]{0:T(128)S(1)}, u32[]{:S(2)}) copy-start(f32[4]{0:T(128)S(1)} %get-tuple-element.433) | copy-start | bytes 52
  7.4 172.3 %copy-start.16 = (f32[3,4,32,256]{3,2,1,0:T(8,128)}, f32[3,4,32,256]{3,2,1,0:T(8,128)S(1)}, u32[]{:S(2)}) copy-start(f32[3,4,32,256]{3,2,1,0:T(8,128)S(1)} %broadcast_multiply_fusion) | copy-start | bytes 1179652
  7.4 165.7 %copy-start.77 = (f32[32]{0:T(128)}, f32[32]{0:T(128)S(1)}, u32[]{:S(2)}) copy-start(f32[32]{0:T(128)S(1)} %get-tuple-element.430) | copy-start | bytes 388
  7.4 165.7 %copy-start.81 = (f32[32]{0:T(128)}, f32[32]{0:T(128)S(1)}, u32[]{:S(2)}) copy-start(f32[32]{0:T(128)S(1)} %get-tuple-element.431) | copy-start | bytes 388
  7.4 6.8 %copy-start = (f32[1,3,2,4,32,256]{5,4,3,2,1,0:T(8,128)S(1)}, f32[1,3,2,4,32,256]{5,4,3,2,1,0:T(8,128)}, u32[]{:S(2)}) copy-start(f32[1,3,2,4,32,256]{5,4,3,2,1,0:T(8,128)} %param.3) | copy-start | bytes 2359300
  15.4 7.2 %collective-permute-start.2 = (f32[1,3,2,4,1,256]{5,4,3,2,1,0:T(1,128)S(1)}, f32[1,3,2,4,1,256]{5,4,3,2,1,0:T(1,128)S(1)}, u32[]{:S(2)}, u32[]{:S(2)}) collective-permute-start(f32[1,3,2,4,1,256]{5,4,3,2,1,0:T(1,128)S(1)} %pad_maximum_fusion.40), channel_id=1, source_target_pairs={{0,1},{2,3},{4,5},{6,7},{8,9},{10,11},{12,13},{14,15},{16,17},{18,... | collective-permute-start | bytes 73736 | tf_op jit(solution)/shard_map/ppermute | solution.py:15
  17.5 8.7 %collective-permute-start.3 = (f32[1,3,2,1,32,256]{5,4,3,2,1,0:T(8,128)S(1)}, f32[1,3,2,1,32,256]{5,4,3,2,1,0:T(8,128)S(1)}, u32[]{:S(2)}, u32[]{:S(2)}) collective-permute-start(f32[1,3,2,1,32,256]{5,4,3,2,1,0:T(8,128)S(1)} %pad_maximum_fusion.33), channel_id=1, source_target_pairs={{0,2},{2,4},{4,6},{6,8},{8,10},{10,12},{12,14},{1,3},{3,5},{5,7},{... | collective-permute-start | bytes 589832 | tf_op jit(solution)/shard_map/ppermute | solution.py:15
  22.5 156.8 %copy-start.69 = (f32[32]{0:T(128)}, f32[32]{0:T(128)S(1)}, u32[]{:S(2)}) copy-start(f32[32]{0:T(128)S(1)} %get-tuple-element.422) | copy-start | bytes 388
  22.5 156.8 %copy-start.73 = (f32[32]{0:T(128)}, f32[32]{0:T(128)S(1)}, u32[]{:S(2)}) copy-start(f32[32]{0:T(128)S(1)} %get-tuple-element.423) | copy-start | bytes 388
  27.5 45.4 %copy-start.27 = (f32[1,3,2,4,32,256]{5,4,3,2,1,0:T(8,128)}, f32[1,3,2,4,32,256]{5,4,3,2,1,0:T(8,128)S(1)}, u32[]{:S(2)}) copy-start(f32[1,3,2,4,32,256]{5,4,3,2,1,0:T(8,128)S(1)} %maximum_subtract_fusion) | copy-start | bytes 2359300
  73.0 7.6 %collective-permute-start.4 = (f32[1,3,2,1,32,256]{5,4,3,2,1,0:T(8,128)S(1)}, f32[1,3,2,1,32,256]{5,4,3,2,1,0:T(8,128)S(1)}, u32[]{:S(2)}, u32[]{:S(2)}) collective-permute-start(f32[1,3,2,1,32,256]{5,4,3,2,1,0:T(8,128)S(1)} %slice.2127), channel_id=1, source_target_pairs={{2,0},{4,2},{6,4},{8,6},{10,8},{12,10},{14,12},{3,1},{5,3},{7,5},{... | collective-permute-start | bytes 589832 | tf_op jit(solution)/shard_map/ppermute | solution.py:15
  74.3 3.1 collective-permute-start.5
  81.7 5.9 %collective-permute-start.7 = (f32[1,3,2,1,32,256]{5,4,3,2,1,0:T(8,128)S(1)}, f32[1,3,2,1,32,256]{5,4,3,2,1,0:T(8,128)S(1)}, u32[]{:S(2)}, u32[]{:S(2)}) collective-permute-start(f32[1,3,2,1,32,256]{5,4,3,2,1,0:T(8,128)S(1)} %pad_maximum_fusion.31), channel_id=1, source_target_pairs={{0,2},{2,4},{4,6},{6,8},{8,10},{10,12},{12,14},{1,3},{3,5},{5,7},{... | collective-permute-start | bytes 589832 | tf_op jit(solution)/shard_map/ppermute | solution.py:15
  83.2 4.4 collective-permute-start.6
  124.4 19.6 %copy-start.29 = (f32[1,3,2,4,32,256]{5,4,3,2,1,0:T(8,128)S(1)}, f32[1,3,2,4,32,256]{5,4,3,2,1,0:T(8,128)}, u32[]{:S(2)}) copy-start(f32[1,3,2,4,32,256]{5,4,3,2,1,0:T(8,128)} %copy-done.28) | copy-start | bytes 2359300
  145.4 34.3 %copy-start.1 = (f32[1,3,1,4,32,256]{5,4,3,2,1,0:T(8,128)}, f32[1,3,1,4,32,256]{5,4,3,2,1,0:T(8,128)S(1)}, u32[]{:S(2)}) copy-start(f32[1,3,1,4,32,256]{5,4,3,2,1,0:T(8,128)S(1)} %get-tuple-element.131) | copy-start | bytes 1179652
  163.5 16.2 %copy-start.34 = (f32[1,3,1,4,32,256]{5,4,3,2,1,0:T(8,128)}, f32[1,3,1,4,32,256]{5,4,3,2,1,0:T(8,128)S(1)}, u32[]{:S(2)}) copy-start(f32[1,3,1,4,32,256]{5,4,3,2,1,0:T(8,128)S(1)} %get-tuple-element.132) | copy-start | bytes 1179652
  163.5 16.2 %copy-start.36 = (f32[1,3,1,4,32,256]{5,4,3,2,1,0:T(8,128)}, f32[1,3,1,4,32,256]{5,4,3,2,1,0:T(8,128)S(1)}, u32[]{:S(2)}) copy-start(f32[1,3,1,4,32,256]{5,4,3,2,1,0:T(8,128)S(1)} %get-tuple-element.133) | copy-start | bytes 1179652
  163.9 9.1 %copy-start.5 = (f32[1,3,2,4,32,256]{5,4,3,2,1,0:T(8,128)}, f32[1,3,2,4,32,256]{5,4,3,2,1,0:T(8,128)S(1)}, u32[]{:S(2)}) copy-start(f32[1,3,2,4,32,256]{5,4,3,2,1,0:T(8,128)S(1)} %maximum_add_fusion.1) | copy-start | bytes 2359300
  163.9 8.6 %collective-permute-start.8 = (f32[1,3,2,1,32,256]{5,4,3,2,1,0:T(8,128)S(1)}, f32[1,3,2,1,32,256]{5,4,3,2,1,0:T(8,128)S(1)}, u32[]{:S(2)}, u32[]{:S(2)}) collective-permute-start(f32[1,3,2,1,32,256]{5,4,3,2,1,0:T(8,128)S(1)} %slice.2170), channel_id=1, source_target_pairs={{2,0},{4,2},{6,4},{8,6},{10,8},{12,10},{14,12},{3,1},{5,3},{7,5},{... | collective-permute-start | bytes 589832 | tf_op jit(solution)/shard_map/ppermute | solution.py:15
  165.2 3.1 collective-permute-start.9
  173.6 4.9 %collective-permute-start.11 = (f32[1,3,2,1,32,256]{5,4,3,2,1,0:T(8,128)S(1)}, f32[1,3,2,1,32,256]{5,4,3,2,1,0:T(8,128)S(1)}, u32[]{:S(2)}, u32[]{:S(2)}) collective-permute-start(f32[1,3,2,1,32,256]{5,4,3,2,1,0:T(8,128)S(1)} %pad_maximum_fusion.29), channel_id=1, source_target_pairs={{0,2},{2,4},{4,6},{6,8},{8,10},{10,12},{12,14},{1,3},{3,5},{5,7},{... | collective-permute-start | bytes 589832 | tf_op jit(solution)/shard_map/ppermute | solution.py:15
  175.1 2.1 collective-permute-start.10
  213.7 11.6 %copy-start.2 = (f32[1,3,1,4,32,256]{5,4,3,2,1,0:T(8,128)S(1)}, f32[1,3,1,4,32,256]{5,4,3,2,1,0:T(8,128)}, u32[]{:S(2)}) copy-start(f32[1,3,1,4,32,256]{5,4,3,2,1,0:T(8,128)} %copy-done.1) | copy-start | bytes 1179652
  225.2 17.0 %copy-start.9 = (f32[1,3,1,4,32,256]{5,4,3,2,1,0:T(8,128)}, f32[1,3,1,4,32,256]{5,4,3,2,1,0:T(8,128)S(1)}, u32[]{:S(2)}) copy-start(f32[1,3,1,4,32,256]{5,4,3,2,1,0:T(8,128)S(1)} %get-tuple-element.118) | copy-start | bytes 1179652
  225.2 17.0 %copy-start.12 = (f32[1,3,1,4,32,256]{5,4,3,2,1,0:T(8,128)}, f32[1,3,1,4,32,256]{5,4,3,2,1,0:T(8,128)S(1)}, u32[]{:S(2)}) copy-start(f32[1,3,1,4,32,256]{5,4,3,2,1,0:T(8,128)S(1)} %get-tuple-element.119) | copy-start | bytes 1179652
  225.6 7.8 %collective-permute-start.12 = (f32[1,3,2,1,32,256]{5,4,3,2,1,0:T(8,128)S(1)}, f32[1,3,2,1,32,256]{5,4,3,2,1,0:T(8,128)S(1)}, u32[]{:S(2)}, u32[]{:S(2)}) collective-permute-start(f32[1,3,2,1,32,256]{5,4,3,2,1,0:T(8,128)S(1)} %slice.2211), channel_id=1, source_target_pairs={{2,0},{4,2},{6,4},{8,6},{10,8},{12,10},{14,12},{3,1},{5,3},{7,5},{... | collective-permute-start | bytes 589832 | tf_op jit(solution)/shard_map/ppermute | solution.py:15
  226.9 3.1 collective-permute-start.13
  235.0 5.6 %collective-permute-start.15 = (f32[1,3,2,1,32,256]{5,4,3,2,1,0:T(8,128)S(1)}, f32[1,3,2,1,32,256]{5,4,3,2,1,0:T(8,128)S(1)}, u32[]{:S(2)}, u32[]{:S(2)}) collective-permute-start(f32[1,3,2,1,32,256]{5,4,3,2,1,0:T(8,128)S(1)} %pad_maximum_fusion.27), channel_id=1, source_target_pairs={{0,2},{2,4},{4,6},{6,8},{8,10},{10,12},{12,14},{1,3},{3,5},{5,7},{... | collective-permute-start | bytes 589832 | tf_op jit(solution)/shard_map/ppermute | solution.py:15
  236.5 4.0 collective-permute-start.14
  281.9 20.7 %copy-start.31 = (f32[1,3,2,4,32,256]{5,4,3,2,1,0:T(8,128)S(1)}, f32[1,3,2,4,32,256]{5,4,3,2,1,0:T(8,128)}, u32[]{:S(2)}) copy-start(f32[1,3,2,4,32,256]{5,4,3,2,1,0:T(8,128)} %copy-done.30) | copy-start | bytes 2359300
  300.0 3.8 copy-start.85
  300.0 21.2 %copy-start.3 = (f32[1,3,1,4,32,256]{5,4,3,2,1,0:T(8,128)S(1)}, f32[1,3,1,4,32,256]{5,4,3,2,1,0:T(8,128)}, u32[]{:S(2)}) copy-start(f32[1,3,1,4,32,256]{5,4,3,2,1,0:T(8,128)} %copy-done.1) | copy-start | bytes 1179652
  300.0 21.2 %copy-start.35 = (f32[1,3,1,4,32,256]{5,4,3,2,1,0:T(8,128)S(1)}, f32[1,3,1,4,32,256]{5,4,3,2,1,0:T(8,128)}, u32[]{:S(2)}) copy-start(f32[1,3,1,4,32,256]{5,4,3,2,1,0:T(8,128)} %copy-done.34) | copy-start | bytes 1179652
  300.0 21.2 %copy-start.37 = (f32[1,3,1,4,32,256]{5,4,3,2,1,0:T(8,128)S(1)}, f32[1,3,1,4,32,256]{5,4,3,2,1,0:T(8,128)}, u32[]{:S(2)}) copy-start(f32[1,3,1,4,32,256]{5,4,3,2,1,0:T(8,128)} %copy-done.36) | copy-start | bytes 1179652
  303.8 36.1 %copy-start.20 = (f32[1,3,1,4,32,256]{5,4,3,2,1,0:T(8,128)}, f32[1,3,1,4,32,256]{5,4,3,2,1,0:T(8,128)S(1)}, u32[]{:S(2)}) copy-start(f32[1,3,1,4,32,256]{5,4,3,2,1,0:T(8,128)S(1)} %get-tuple-element.100) | copy-start | bytes 1179652
  303.8 36.1 %copy-start.23 = (f32[1,3,1,4,32,256]{5,4,3,2,1,0:T(8,128)}, f32[1,3,1,4,32,256]{5,4,3,2,1,0:T(8,128)S(1)}, u32[]{:S(2)}) copy-start(f32[1,3,1,4,32,256]{5,4,3,2,1,0:T(8,128)S(1)} %get-tuple-element.101) | copy-start | bytes 1179652
  323.2 8.7 %copy-start.7 = (f32[1,3,2,4,32,256]{5,4,3,2,1,0:T(8,128)}, f32[1,3,2,4,32,256]{5,4,3,2,1,0:T(8,128)S(1)}, u32[]{:S(2)}) copy-start(f32[1,3,2,4,32,256]{5,4,3,2,1,0:T(8,128)S(1)} %maximum_add_fusion.2) | copy-start | bytes 2359300
  323.3 8.1 %collective-permute-start.16 = (f32[1,3,2,1,32,256]{5,4,3,2,1,0:T(8,128)S(1)}, f32[1,3,2,1,32,256]{5,4,3,2,1,0:T(8,128)S(1)}, u32[]{:S(2)}, u32[]{:S(2)}) collective-permute-start(f32[1,3,2,1,32,256]{5,4,3,2,1,0:T(8,128)S(1)} %slice.2254), channel_id=1, source_target_pairs={{2,0},{4,2},{6,4},{8,6},{10,8},{12,10},{14,12},{3,1},{5,3},{7,5},{... | collective-permute-start | bytes 589832 | tf_op jit(solution)/shard_map/ppermute | solution.py:15
  324.6 3.1 collective-permute-start.17
  333.0 5.3 %collective-permute-start.19 = (f32[1,3,2,1,32,256]{5,4,3,2,1,0:T(8,128)S(1)}, f32[1,3,2,1,32,256]{5,4,3,2,1,0:T(8,128)S(1)}, u32[]{:S(2)}, u32[]{:S(2)}) collective-permute-start(f32[1,3,2,1,32,256]{5,4,3,2,1,0:T(8,128)S(1)} %pad_maximum_fusion.25), channel_id=1, source_target_pairs={{0,2},{2,4},{4,6},{6,8},{8,10},{10,12},{12,14},{1,3},{3,5},{5,7},{... | collective-permute-start | bytes 589832 | tf_op jit(solution)/shard_map/ppermute | solution.py:15
  334.6 2.1 collective-permute-start.18
  390.6 23.8 %copy-start.38 = (f32[1,3,1,4,32,256]{5,4,3,2,1,0:T(8,128)}, f32[1,3,1,4,32,256]{5,4,3,2,1,0:T(8,128)S(1)}, u32[]{:S(2)}) copy-start(f32[1,3,1,4,32,256]{5,4,3,2,1,0:T(8,128)S(1)} %get-tuple-element.86) | copy-start | bytes 1179652
  390.7 23.8 %copy-start.40 = (f32[1,3,1,4,32,256]{5,4,3,2,1,0:T(8,128)}, f32[1,3,1,4,32,256]{5,4,3,2,1,0:T(8,128)S(1)}, u32[]{:S(2)}) copy-start(f32[1,3,1,4,32,256]{5,4,3,2,1,0:T(8,128)S(1)} %get-tuple-element.87) | copy-start | bytes 1179652
  390.7 4.9 %copy-start.6 = (f32[1,3,2,4,32,256]{5,4,3,2,1,0:T(8,128)S(1)}, f32[1,3,2,4,32,256]{5,4,3,2,1,0:T(8,128)}, u32[]{:S(2)}) copy-start(f32[1,3,2,4,32,256]{5,4,3,2,1,0:T(8,128)} %copy-done.5) | copy-start | bytes 2359300
  393.0 5.0 %collective-permute-start.21 = (f32[1,3,2,4,1,256]{5,4,3,2,1,0:T(1,128)S(1)}, f32[1,3,2,4,1,256]{5,4,3,2,1,0:T(1,128)S(1)}, u32[]{:S(2)}, u32[]{:S(2)}) collective-permute-start(f32[1,3,2,4,1,256]{5,4,3,2,1,0:T(1,128)S(1)} %slice.2299), channel_id=1, source_target_pairs={{1,0},{3,2},{5,4},{7,6},{9,8},{11,10},{13,12},{15,14},{17,16},{19,... | collective-permute-start | bytes 73736 | tf_op jit(solution)/shard_map/ppermute | solution.py:15
  394.3 9.5 %collective-permute-start.20 = (f32[1,3,2,1,32,256]{5,4,3,2,1,0:T(8,128)S(1)}, f32[1,3,2,1,32,256]{5,4,3,2,1,0:T(8,128)S(1)}, u32[]{:S(2)}, u32[]{:S(2)}) collective-permute-start(f32[1,3,2,1,32,256]{5,4,3,2,1,0:T(8,128)S(1)} %slice.2295), channel_id=1, source_target_pairs={{2,0},{4,2},{6,4},{8,6},{10,8},{12,10},{14,12},{3,1},{5,3},{7,5},{... | collective-permute-start | bytes 589832 | tf_op jit(solution)/shard_map/ppermute | solution.py:15
  405.4 6.1 %collective-permute-start.22 = (f32[1,3,2,4,1,256]{5,4,3,2,1,0:T(1,128)S(1)}, f32[1,3,2,4,1,256]{5,4,3,2,1,0:T(1,128)S(1)}, u32[]{:S(2)}, u32[]{:S(2)}) collective-permute-start(f32[1,3,2,4,1,256]{5,4,3,2,1,0:T(1,128)S(1)} %pad_maximum_fusion.35), channel_id=1, source_target_pairs={{0,1},{2,3},{4,5},{6,7},{8,9},{10,11},{12,13},{14,15},{16,17},{18,... | collective-permute-start | bytes 73736 | tf_op jit(solution)/shard_map/ppermute | solution.py:15
  407.5 5.3 %collective-permute-start.23 = (f32[1,3,2,1,32,256]{5,4,3,2,1,0:T(8,128)S(1)}, f32[1,3,2,1,32,256]{5,4,3,2,1,0:T(8,128)S(1)}, u32[]{:S(2)}, u32[]{:S(2)}) collective-permute-start(f32[1,3,2,1,32,256]{5,4,3,2,1,0:T(8,128)S(1)} %pad_maximum_fusion.23), channel_id=1, source_target_pairs={{0,2},{2,4},{4,6},{6,8},{8,10},{10,12},{12,14},{1,3},{3,5},{5,7},{... | collective-permute-start | bytes 589832 | tf_op jit(solution)/shard_map/ppermute | solution.py:15
  417.3 3.3 copy-start.8
  461.4 4.0 copy-start.15
  461.4 4.0 copy-start.22
  461.4 4.1 copy-start.25
  461.4 4.1 copy-start.39
  461.4 4.1 copy-start.41
  465.6 2.1 copy-start.49
  465.6 2.2 copy-start.50
  465.6 2.3 copy-start.51
  (46 other events, 43.2 us)
where the time goes:
time: 472 us; the launch traced here: 469 us
  blocking collectives  181 us (38%)
  between operations  99.9 us (21%)
  other arithmetic  74.5 us (16%)
  waiting for transfers between devices  43.6 us (9%)
  starting transfers between devices  38.4 us (8%)
  local copies, waits for them, and re-layouts  31.8 us (7%)
    psum x3, blocking collectives, body(): lax.psum((product(second, middle), product(second, second), product(sourc...  89.6 us
    psum x2, blocking collectives, body(): lax.psum(product(source, applied), ('gx', 'gy'))  60.3 us
    ppermute x24, waiting for transfers between devices, shifted(): return lax.ppermute(array, axis, pairs)  43.6 us
    ppermute x24, starting transfers between devices, shifted(): return lax.ppermute(array, axis, pairs)  38.4 us
    psum x1, blocking collectives, body(): shadow_dot = lax.psum(product(source, residual), ('gx', 'gy'))  31.3 us
    sub x15, other arithmetic, scaled(): real_part = values[:, :, 0] * real_scale - values[:, :, 1] * imag_scale  27.3 us
    another operation x12, other arithmetic, product(): return jnp.stack([real_part, imag_part])  17.5 us
    unnamed x173, local copies, waits for them, and re-layouts  12.9 us
  transfers between devices with their start and end apart: 24, of which 17 were waited for; matrix products, arithmetic and copies ran while one was open for 2% of the time, Pallas kernels for 0%

commit v1 on v0

--- a/solution.py
+++ b/solution.py
@@ -151,7 +151,9 @@
     solution = jnp.zeros_like(source)
     residual = source
     direction = source
-    shadow_dot = lax.psum(product(source, residual), ("gx", "gy"))
+    state = product(source, residual)
+    current_arr = lax.all_gather(state, axis_name=("gx", "gy"))
+    shadow_dot = jnp.sum(current_arr, axis=0)
     for iteration in range(ITERS):
         applied = operate(direction)
         step_size = complex_ratio(shadow_dot, lax.psum(product(source, applied), ("gx", "gy")))

time: 472 us -> 475 us (level)
    psum x1 -> x0, blocking collectives: 31.3 us -> none  [body(): shadow_dot = lax.psum(product(source, residual), ('gx', 'gy'))]
    unnamed x0 -> x1, blocking collectives: none -> 31.2 us
    unnamed x173 -> x193, local copies, waits for them, and re-layouts: 12.9 us -> 15.4 us
    another operation x12 -> x11, other arithmetic: 17.5 us -> 16 us  [product(): return jnp.stack([real_part, imag_part])]
where the time goes in v1:
time: 475 us; the launch traced here: 472 us
  blocking collectives  181 us (38%)
  between operations  99.5 us (21%)
  other arithmetic  76.3 us (16%)
  waiting for transfers between devices  41.5 us (9%)
  starting transfers between devices  38.4 us (8%)
  local copies, waits for them, and re-layouts  35.3 us (7%)
    psum x3, blocking collectives, body(): lax.psum((product(second, middle), product(second, second), product(sourc...  89.6 us
    psum x2, blocking collectives, body(): lax.psum(product(source, applied), ('gx', 'gy'))  60.3 us
    ppermute x24, waiting for transfers between devices, shifted(): return lax.ppermute(array, axis, pairs)  41.5 us
    ppermute x24, starting transfers between devices, shifted(): return lax.ppermute(array, axis, pairs)  38.4 us
    unnamed x1, blocking collectives  31.2 us
    sub x15, other arithmetic, scaled(): real_part = values[:, :, 0] * real_scale - values[:, :, 1] * imag_scale  27.6 us
    another operation x11, other arithmetic, product(): return jnp.stack([real_part, imag_part])  16 us
    unnamed x193, local copies, waits for them, and re-layouts  15.4 us
  transfers between devices with their start and end apart: 24, of which 17 were waited for; matrix products, arithmetic and copies ran while one was open for 2% of the time, Pallas kernels for 0%

profile of v1, /device:TPU:0, one launch (start us, length us, event | category | flops | bytes accessed | tf_op | source)
XLA Modules:
  0.0 472.0 jit_solution(14484255249574176687)
XLA Ops:
  1.6 1.3 collective-permute-start.1
  3.9 1.3 collective-permute-start
  8.0 6.1 %collective-permute-done = f32[1,3,2,1,32,256]{5,4,3,2,1,0:T(8,128)S(1)} collective-permute-done((f32[1,3,2,1,32,256]{5,4,3,2,1,0:T(8,128)S(1)}, f32[1,3,2,1,32,256]{5,4,3,2,1,0:T(8,128)S(1)}, u32[]{:S(2)}, u32[]{:S(2)}) %collective-permute-start) | collective-permute-done | bytes 196640 | tf_op jit(solution)/shard_map/ppermute | solution.py:15
  16.4 2.1 collective-permute-start.2
  18.6 5.0 %collective-permute-start.3 = (f32[1,3,2,1,32,256]{5,4,3,2,1,0:T(8,128)}, f32[1,3,2,1,32,256]{5,4,3,2,1,0:T(8,128)S(1)}, u32[]{:S(2)}, u32[]{:S(2)}) collective-permute-start(f32[1,3,2,1,32,256]{5,4,3,2,1,0:T(8,128)} %pad_maximum_fusion.33), channel_id=1, source_target_pairs={{0,2},{2,4},{4,6},{6,8},{8,10},{10,12},{12,14},{1,3},{3,5},{5,7},{... | collective-permute-start | bytes 589832 | tf_op jit(solution)/shard_map/ppermute | solution.py:15
  25.4 2.2 collective-permute-done.3
  33.4 1.4 fusion.75
  34.8 31.2 %all-reduce.40 = (f32[32]{0:T(128)S(1)}, f32[2,1]{1,0:T(2,128)S(1)}) all-reduce(f32[32]{0:T(128)S(1)} %fusion.75, f32[2,1]{1,0:T(2,128)S(1)} %pad_maximum_fusion.41), channel_id=2, replica_groups=mesh['groups'=2,'gx'=8,'gy'=2] {'gx','gy'}, use_global_device_ids=true, to_apply=%add.36 | all-reduce | flops 34 | bytes 272
  75.3 1.3 multiply_subtract_fusion.14
  76.8 1.3 collective-permute-start.4
  78.2 1.3 collective-permute-start.5
  79.5 1.8 collective-permute-done.5
  81.3 3.2 collective-permute-done.4
  86.0 1.5 collective-permute-start.7
  87.5 1.7 collective-permute-start.6
  99.2 29.5 %all-reduce.39 = (f32[2,1]{1,0:T(2,128)S(1)}, f32[2,1]{1,0:T(2,128)S(1)}, f32[2,1]{1,0:T(2,128)S(1)}) all-reduce(f32[2,1]{1,0:T(2,128)S(1)} %pad_maximum_fusion.42, f32[2,1]{1,0:T(2,128)S(1)} %pad_maximum_fusion.43, f32[2,1]{1,0:T(2,128)S(1)} %pad_maximum_fusion.44), channel_id=1, replica_groups=mesh['groups'=2,'gx'=8,'gy'=2] {'gx','gy'}, use_global_device_ids=true, to_apply=%region_8.0 | all-reduce | flops 6 | bytes 48 | tf_op jit(solution)/shard_map/psum | solution.py:162
  145.3 2.5 multiply_subtract_fusion.11
  147.8 1.3 multiply_subtract_fusion.12
  167.6 1.3 collective-permute-start.8
  168.9 1.3 collective-permute-start.9
  170.2 1.8 collective-permute-done.9
  172.0 4.1 collective-permute-done.8
  177.3 1.5 collective-permute-start.11
  185.6 1.3 pad_maximum_fusion.45
  187.0 30.3 %psum.81 = f32[2,1]{1,0:T(2,128)S(1)} all-reduce(f32[2,1]{1,0:T(2,128)S(1)} %pad_maximum_fusion.45), channel_id=1, replica_groups=mesh['groups'=2,'gx'=8,'gy'=2] {'gx','gy'}, use_global_device_ids=true, to_apply=%region_17.0 | all-reduce | flops 2 | bytes 16 | tf_op jit(solution)/shard_map/psum | solution.py:159
  226.1 2.6 multiply_subtract_fusion.8
  229.1 1.3 collective-permute-start.12
  230.4 1.5 collective-permute-start.13
  231.9 1.6 collective-permute-done.13
  233.5 3.4 collective-permute-done.12
  238.5 1.5 collective-permute-start.15
  240.0 1.5 collective-permute-start.14
  249.2 1.8 pad_maximum_fusion.48
  250.9 1.8 pad_maximum_fusion.47
  252.7 1.8 pad_maximum_fusion.46
  254.5 30.6 %all-reduce.38 = (f32[2,1]{1,0:T(2,128)}, f32[2,1]{1,0:T(2,128)}, f32[2,1]{1,0:T(2,128)}) all-reduce(f32[2,1]{1,0:T(2,128)} %pad_maximum_fusion.46, f32[2,1]{1,0:T(2,128)} %pad_maximum_fusion.47, f32[2,1]{1,0:T(2,128)} %pad_maximum_fusion.48), channel_id=1, replica_groups=mesh['groups'=2,'gx'=8,'gy'=2] {'gx','gy'}, use_global_device_ids=true, to_apply=%region_20.0 | all-reduce | flops 6 | bytes 48 | tf_op jit(solution)/shard_map/psum | solution.py:162
  285.1 1.3 fusion.89
  302.9 2.5 multiply_subtract_fusion.5
  305.5 1.3 multiply_subtract_fusion.6
  326.0 1.3 collective-permute-start.16
  327.3 1.3 collective-permute-start.17
  328.6 1.8 collective-permute-done.17
  330.4 3.7 collective-permute-done.16
  335.8 1.5 collective-permute-start.19
  339.4 1.7 collective-permute-done.19
  345.1 2.9 add_reduce_fusion.2
  348.0 1.8 pad_maximum_fusion.49
  349.8 2.2 multiply_subtract_fusion.13
  352.1 30.0 %psum.85 = f32[2,1]{1,0:T(2,128)S(1)} all-reduce(f32[2,1]{1,0:T(2,128)} %pad_maximum_fusion.49), channel_id=1, replica_groups=mesh['groups'=2,'gx'=8,'gy'=2] {'gx','gy'}, use_global_device_ids=true, to_apply=%region_29.0 | all-reduce | flops 2 | bytes 16 | tf_op jit(solution)/shard_map/psum | solution.py:159
  390.5 2.5 multiply_subtract_fusion.2
  393.1 2.3 maximum_subtract_fusion.11
  395.4 1.3 collective-permute-start.21
  396.7 1.3 collective-permute-start.20
  398.0 2.4 multiply_subtract_fusion.9
  400.4 5.8 %collective-permute-done.20 = f32[1,3,2,1,32,256]{5,4,3,2,1,0:T(8,128)S(1)} collective-permute-done((f32[1,3,2,1,32,256]{5,4,3,2,1,0:T(8,128)S(1)}, f32[1,3,2,1,32,256]{5,4,3,2,1,0:T(8,128)S(1)}, u32[]{:S(2)}, u32[]{:S(2)}) %collective-permute-start.20) | collective-permute-done | bytes 196640 | tf_op jit(solution)/shard_map/ppermute | solution.py:15
  407.9 2.0 collective-permute-start.22
  409.9 1.9 collective-permute-start.23
  411.8 2.3 multiply_subtract_fusion.7
  423.3 2.3 multiply_subtract_fusion.3
  425.6 29.5 %all-reduce.37 = (f32[2,1]{1,0:T(2,128)S(1)}, f32[2,1]{1,0:T(2,128)S(1)}) all-reduce(f32[2,1]{1,0:T(2,128)S(1)} %pad_maximum_fusion.50, f32[2,1]{1,0:T(2,128)S(1)} %pad_maximum_fusion.51), channel_id=1, replica_groups=mesh['groups'=2,'gx'=8,'gy'=2] {'gx','gy'}, use_global_device_ids=true, to_apply=%region_32.0 | all-reduce | flops 4 | bytes 32 | tf_op jit(solution)/shard_map/psum | solution.py:162
  464.1 2.7 multiply_subtract_fusion
  466.8 1.4 multiply_subtract_fusion.1
  468.3 1.5 maximum_subtract_fusion.13
  470.6 1.4 fusion.3
  (445 shorter events, 71.9 us)
Async XLA Ops:
  0.6 7.3 %copy-start.56 = (f32[3,4,32,256]{3,2,1,0:T(8,128)S(1)}, f32[3,4,32,256]{3,2,1,0:T(8,128)}, u32[]{:S(2)}) copy-start(f32[3,4,32,256]{3,2,1,0:T(8,128)} %param.4) | copy-start | bytes 1179652
  1.6 12.5 %collective-permute-start.1 = (f32[1,3,2,4,1,256]{5,4,3,2,1,0:T(1,128)S(1)}, f32[1,3,2,4,1,256]{5,4,3,2,1,0:T(1,128)S(1)}, u32[]{:S(2)}, u32[]{:S(2)}) collective-permute-start(f32[1,3,2,4,1,256]{5,4,3,2,1,0:T(1,128)S(1)} %slice.704), channel_id=1, source_target_pairs={{1,0},{3,2},{5,4},{7,6},{9,8},{11,10},{13,12},{15,14},{17,16},{19,... | collective-permute-start | bytes 73736 | tf_op jit(solution)/shard_map/ppermute | solution.py:15
  3.9 10.2 %collective-permute-start = (f32[1,3,2,1,32,256]{5,4,3,2,1,0:T(8,128)S(1)}, f32[1,3,2,1,32,256]{5,4,3,2,1,0:T(8,128)S(1)}, u32[]{:S(2)}, u32[]{:S(2)}) collective-permute-start(f32[1,3,2,1,32,256]{5,4,3,2,1,0:T(8,128)S(1)} %slice.697), channel_id=1, source_target_pairs={{2,0},{4,2},{6,4},{8,6},{10,8},{12,10},{14,12},{3,1},{5,3},{7,5},{... | collective-permute-start | bytes 589832 | tf_op jit(solution)/shard_map/ppermute | solution.py:15
  7.7 7.2 %copy-start.65 = (f32[4]{0:T(128)}, f32[4]{0:T(128)S(1)}, u32[]{:S(2)}) copy-start(f32[4]{0:T(128)S(1)} %get-tuple-element.430) | copy-start | bytes 52
  7.7 7.2 %copy-start.70 = (f32[4]{0:T(128)}, f32[4]{0:T(128)S(1)}, u32[]{:S(2)}) copy-start(f32[4]{0:T(128)S(1)} %get-tuple-element.431) | copy-start | bytes 52
  8.0 175.3 %copy-start.16 = (f32[3,4,32,256]{3,2,1,0:T(8,128)}, f32[3,4,32,256]{3,2,1,0:T(8,128)S(1)}, u32[]{:S(2)}) copy-start(f32[3,4,32,256]{3,2,1,0:T(8,128)S(1)} %broadcast_multiply_fusion) | copy-start | bytes 1179652
  8.0 7.2 %copy-start.83 = (f32[32]{0:T(128)}, f32[32]{0:T(128)S(1)}, u32[]{:S(2)}) copy-start(f32[32]{0:T(128)S(1)} %get-tuple-element.428) | copy-start | bytes 388
  8.0 7.2 %copy-start.88 = (f32[32]{0:T(128)}, f32[32]{0:T(128)S(1)}, u32[]{:S(2)}) copy-start(f32[32]{0:T(128)S(1)} %get-tuple-element.429) | copy-start | bytes 388
  8.0 6.3 %copy-start = (f32[1,3,2,4,32,256]{5,4,3,2,1,0:T(8,128)S(1)}, f32[1,3,2,4,32,256]{5,4,3,2,1,0:T(8,128)}, u32[]{:S(2)}) copy-start(f32[1,3,2,4,32,256]{5,4,3,2,1,0:T(8,128)} %param.3) | copy-start | bytes 2359300
  15.7 8.5 %copy-start.94 = (u32[32]{0:T(128)S(1)}, u32[32]{0:T(128)}, u32[]{:S(2)}) copy-start(u32[32]{0:T(128)} %constant.136) | copy-start | bytes 388
  16.4 9.0 %collective-permute-start.2 = (f32[1,3,2,4,1,256]{5,4,3,2,1,0:T(1,128)S(1)}, f32[1,3,2,4,1,256]{5,4,3,2,1,0:T(1,128)S(1)}, u32[]{:S(2)}, u32[]{:S(2)}) collective-permute-start(f32[1,3,2,4,1,256]{5,4,3,2,1,0:T(1,128)S(1)} %pad_maximum_fusion.40), channel_id=1, source_target_pairs={{0,1},{2,3},{4,5},{6,7},{8,9},{10,11},{12,13},{14,15},{16,17},{18,... | collective-permute-start | bytes 73736 | tf_op jit(solution)/shard_map/ppermute | solution.py:15
  18.6 9.0 %collective-permute-start.3 = (f32[1,3,2,1,32,256]{5,4,3,2,1,0:T(8,128)}, f32[1,3,2,1,32,256]{5,4,3,2,1,0:T(8,128)S(1)}, u32[]{:S(2)}, u32[]{:S(2)}) collective-permute-start(f32[1,3,2,1,32,256]{5,4,3,2,1,0:T(8,128)} %pad_maximum_fusion.33), channel_id=1, source_target_pairs={{0,2},{2,4},{4,6},{6,8},{8,10},{10,12},{12,14},{1,3},{3,5},{5,7},{... | collective-permute-start | bytes 589832 | tf_op jit(solution)/shard_map/ppermute | solution.py:15
  31.0 45.7 %copy-start.27 = (f32[1,3,2,4,32,256]{5,4,3,2,1,0:T(8,128)}, f32[1,3,2,4,32,256]{5,4,3,2,1,0:T(8,128)S(1)}, u32[]{:S(2)}) copy-start(f32[1,3,2,4,32,256]{5,4,3,2,1,0:T(8,128)S(1)} %maximum_subtract_fusion) | copy-start | bytes 2359300
  76.8 7.6 %collective-permute-start.4 = (f32[1,3,2,1,32,256]{5,4,3,2,1,0:T(8,128)S(1)}, f32[1,3,2,1,32,256]{5,4,3,2,1,0:T(8,128)S(1)}, u32[]{:S(2)}, u32[]{:S(2)}) collective-permute-start(f32[1,3,2,1,32,256]{5,4,3,2,1,0:T(8,128)S(1)} %slice.2129), channel_id=1, source_target_pairs={{2,0},{4,2},{6,4},{8,6},{10,8},{12,10},{14,12},{3,1},{5,3},{7,5},{... | collective-permute-start | bytes 589832 | tf_op jit(solution)/shard_map/ppermute | solution.py:15
  78.2 3.1 collective-permute-start.5
  86.0 6.0 %collective-permute-start.7 = (f32[1,3,2,1,32,256]{5,4,3,2,1,0:T(8,128)S(1)}, f32[1,3,2,1,32,256]{5,4,3,2,1,0:T(8,128)S(1)}, u32[]{:S(2)}, u32[]{:S(2)}) collective-permute-start(f32[1,3,2,1,32,256]{5,4,3,2,1,0:T(8,128)S(1)} %pad_maximum_fusion.31), channel_id=1, source_target_pairs={{0,2},{2,4},{4,6},{6,8},{8,10},{10,12},{12,14},{1,3},{3,5},{5,7},{... | collective-permute-start | bytes 589832 | tf_op jit(solution)/shard_map/ppermute | solution.py:15
  87.5 4.5 collective-permute-start.6
  128.7 19.0 %copy-start.29 = (f32[1,3,2,4,32,256]{5,4,3,2,1,0:T(8,128)S(1)}, f32[1,3,2,4,32,256]{5,4,3,2,1,0:T(8,128)}, u32[]{:S(2)}) copy-start(f32[1,3,2,4,32,256]{5,4,3,2,1,0:T(8,128)} %copy-done.28) | copy-start | bytes 2359300
  149.1 34.2 %copy-start.1 = (f32[1,3,1,4,32,256]{5,4,3,2,1,0:T(8,128)}, f32[1,3,1,4,32,256]{5,4,3,2,1,0:T(8,128)S(1)}, u32[]{:S(2)}) copy-start(f32[1,3,1,4,32,256]{5,4,3,2,1,0:T(8,128)S(1)} %get-tuple-element.131) | copy-start | bytes 1179652
  167.2 16.1 %copy-start.34 = (f32[1,3,1,4,32,256]{5,4,3,2,1,0:T(8,128)}, f32[1,3,1,4,32,256]{5,4,3,2,1,0:T(8,128)S(1)}, u32[]{:S(2)}) copy-start(f32[1,3,1,4,32,256]{5,4,3,2,1,0:T(8,128)S(1)} %get-tuple-element.132) | copy-start | bytes 1179652
  167.2 16.1 %copy-start.36 = (f32[1,3,1,4,32,256]{5,4,3,2,1,0:T(8,128)}, f32[1,3,1,4,32,256]{5,4,3,2,1,0:T(8,128)S(1)}, u32[]{:S(2)}) copy-start(f32[1,3,1,4,32,256]{5,4,3,2,1,0:T(8,128)S(1)} %get-tuple-element.133) | copy-start | bytes 1179652
  167.5 9.1 %copy-start.5 = (f32[1,3,2,4,32,256]{5,4,3,2,1,0:T(8,128)}, f32[1,3,2,4,32,256]{5,4,3,2,1,0:T(8,128)S(1)}, u32[]{:S(2)}) copy-start(f32[1,3,2,4,32,256]{5,4,3,2,1,0:T(8,128)S(1)} %maximum_add_fusion.1) | copy-start | bytes 2359300
  167.6 8.6 %collective-permute-start.8 = (f32[1,3,2,1,32,256]{5,4,3,2,1,0:T(8,128)S(1)}, f32[1,3,2,1,32,256]{5,4,3,2,1,0:T(8,128)S(1)}, u32[]{:S(2)}, u32[]{:S(2)}) collective-permute-start(f32[1,3,2,1,32,256]{5,4,3,2,1,0:T(8,128)S(1)} %slice.2172), channel_id=1, source_target_pairs={{2,0},{4,2},{6,4},{8,6},{10,8},{12,10},{14,12},{3,1},{5,3},{7,5},{... | collective-permute-start | bytes 589832 | tf_op jit(solution)/shard_map/ppermute | solution.py:15
  168.9 3.1 collective-permute-start.9
  177.3 4.9 %collective-permute-start.11 = (f32[1,3,2,1,32,256]{5,4,3,2,1,0:T(8,128)S(1)}, f32[1,3,2,1,32,256]{5,4,3,2,1,0:T(8,128)S(1)}, u32[]{:S(2)}, u32[]{:S(2)}) collective-permute-start(f32[1,3,2,1,32,256]{5,4,3,2,1,0:T(8,128)S(1)} %pad_maximum_fusion.29), channel_id=1, source_target_pairs={{0,2},{2,4},{4,6},{6,8},{8,10},{10,12},{12,14},{1,3},{3,5},{5,7},{... | collective-permute-start | bytes 589832 | tf_op jit(solution)/shard_map/ppermute | solution.py:15
  178.8 2.1 collective-permute-start.10
  217.2 11.5 %copy-start.2 = (f32[1,3,1,4,32,256]{5,4,3,2,1,0:T(8,128)S(1)}, f32[1,3,1,4,32,256]{5,4,3,2,1,0:T(8,128)}, u32[]{:S(2)}) copy-start(f32[1,3,1,4,32,256]{5,4,3,2,1,0:T(8,128)} %copy-done.1) | copy-start | bytes 1179652
  228.7 17.0 %copy-start.9 = (f32[1,3,1,4,32,256]{5,4,3,2,1,0:T(8,128)}, f32[1,3,1,4,32,256]{5,4,3,2,1,0:T(8,128)S(1)}, u32[]{:S(2)}) copy-start(f32[1,3,1,4,32,256]{5,4,3,2,1,0:T(8,128)S(1)} %get-tuple-element.118) | copy-start | bytes 1179652
  228.7 17.0 %copy-start.12 = (f32[1,3,1,4,32,256]{5,4,3,2,1,0:T(8,128)}, f32[1,3,1,4,32,256]{5,4,3,2,1,0:T(8,128)S(1)}, u32[]{:S(2)}) copy-start(f32[1,3,1,4,32,256]{5,4,3,2,1,0:T(8,128)S(1)} %get-tuple-element.119) | copy-start | bytes 1179652
  229.1 7.8 %collective-permute-start.12 = (f32[1,3,2,1,32,256]{5,4,3,2,1,0:T(8,128)S(1)}, f32[1,3,2,1,32,256]{5,4,3,2,1,0:T(8,128)S(1)}, u32[]{:S(2)}, u32[]{:S(2)}) collective-permute-start(f32[1,3,2,1,32,256]{5,4,3,2,1,0:T(8,128)S(1)} %slice.2213), channel_id=1, source_target_pairs={{2,0},{4,2},{6,4},{8,6},{10,8},{12,10},{14,12},{3,1},{5,3},{7,5},{... | collective-permute-start | bytes 589832 | tf_op jit(solution)/shard_map/ppermute | solution.py:15
  230.4 3.1 collective-permute-start.13
  238.5 5.7 %collective-permute-start.15 = (f32[1,3,2,1,32,256]{5,4,3,2,1,0:T(8,128)S(1)}, f32[1,3,2,1,32,256]{5,4,3,2,1,0:T(8,128)S(1)}, u32[]{:S(2)}, u32[]{:S(2)}) collective-permute-start(f32[1,3,2,1,32,256]{5,4,3,2,1,0:T(8,128)S(1)} %pad_maximum_fusion.27), channel_id=1, source_target_pairs={{0,2},{2,4},{4,6},{6,8},{8,10},{10,12},{12,14},{1,3},{3,5},{5,7},{... | collective-permute-start | bytes 589832 | tf_op jit(solution)/shard_map/ppermute | solution.py:15
  240.0 3.9 collective-permute-start.14
  285.1 20.4 %copy-start.31 = (f32[1,3,2,4,32,256]{5,4,3,2,1,0:T(8,128)S(1)}, f32[1,3,2,4,32,256]{5,4,3,2,1,0:T(8,128)}, u32[]{:S(2)}) copy-start(f32[1,3,2,4,32,256]{5,4,3,2,1,0:T(8,128)} %copy-done.30) | copy-start | bytes 2359300
  302.9 3.9 copy-start.93
  302.9 21.0 %copy-start.3 = (f32[1,3,1,4,32,256]{5,4,3,2,1,0:T(8,128)S(1)}, f32[1,3,1,4,32,256]{5,4,3,2,1,0:T(8,128)}, u32[]{:S(2)}) copy-start(f32[1,3,1,4,32,256]{5,4,3,2,1,0:T(8,128)} %copy-done.1) | copy-start | bytes 1179652
  302.9 21.0 %copy-start.35 = (f32[1,3,1,4,32,256]{5,4,3,2,1,0:T(8,128)S(1)}, f32[1,3,1,4,32,256]{5,4,3,2,1,0:T(8,128)}, u32[]{:S(2)}) copy-start(f32[1,3,1,4,32,256]{5,4,3,2,1,0:T(8,128)} %copy-done.34) | copy-start | bytes 1179652
  302.9 21.0 %copy-start.37 = (f32[1,3,1,4,32,256]{5,4,3,2,1,0:T(8,128)S(1)}, f32[1,3,1,4,32,256]{5,4,3,2,1,0:T(8,128)}, u32[]{:S(2)}) copy-start(f32[1,3,1,4,32,256]{5,4,3,2,1,0:T(8,128)} %copy-done.36) | copy-start | bytes 1179652
  306.8 35.9 %copy-start.20 = (f32[1,3,1,4,32,256]{5,4,3,2,1,0:T(8,128)}, f32[1,3,1,4,32,256]{5,4,3,2,1,0:T(8,128)S(1)}, u32[]{:S(2)}) copy-start(f32[1,3,1,4,32,256]{5,4,3,2,1,0:T(8,128)S(1)} %get-tuple-element.100) | copy-start | bytes 1179652
  306.8 35.9 %copy-start.23 = (f32[1,3,1,4,32,256]{5,4,3,2,1,0:T(8,128)}, f32[1,3,1,4,32,256]{5,4,3,2,1,0:T(8,128)S(1)}, u32[]{:S(2)}) copy-start(f32[1,3,1,4,32,256]{5,4,3,2,1,0:T(8,128)S(1)} %get-tuple-element.101) | copy-start | bytes 1179652
  326.0 8.7 %copy-start.7 = (f32[1,3,2,4,32,256]{5,4,3,2,1,0:T(8,128)}, f32[1,3,2,4,32,256]{5,4,3,2,1,0:T(8,128)S(1)}, u32[]{:S(2)}) copy-start(f32[1,3,2,4,32,256]{5,4,3,2,1,0:T(8,128)S(1)} %maximum_add_fusion.2) | copy-start | bytes 2359300
  326.0 8.1 %collective-permute-start.16 = (f32[1,3,2,1,32,256]{5,4,3,2,1,0:T(8,128)S(1)}, f32[1,3,2,1,32,256]{5,4,3,2,1,0:T(8,128)S(1)}, u32[]{:S(2)}, u32[]{:S(2)}) collective-permute-start(f32[1,3,2,1,32,256]{5,4,3,2,1,0:T(8,128)S(1)} %slice.2256), channel_id=1, source_target_pairs={{2,0},{4,2},{6,4},{8,6},{10,8},{12,10},{14,12},{3,1},{5,3},{7,5},{... | collective-permute-start | bytes 589832 | tf_op jit(solution)/shard_map/ppermute | solution.py:15
  327.3 3.1 collective-permute-start.17
  335.8 5.3 %collective-permute-start.19 = (f32[1,3,2,1,32,256]{5,4,3,2,1,0:T(8,128)S(1)}, f32[1,3,2,1,32,256]{5,4,3,2,1,0:T(8,128)S(1)}, u32[]{:S(2)}, u32[]{:S(2)}) collective-permute-start(f32[1,3,2,1,32,256]{5,4,3,2,1,0:T(8,128)S(1)} %pad_maximum_fusion.25), channel_id=1, source_target_pairs={{0,2},{2,4},{4,6},{6,8},{8,10},{10,12},{12,14},{1,3},{3,5},{5,7},{... | collective-permute-start | bytes 589832 | tf_op jit(solution)/shard_map/ppermute | solution.py:15
  337.3 2.1 collective-permute-start.18
  393.1 23.8 %copy-start.38 = (f32[1,3,1,4,32,256]{5,4,3,2,1,0:T(8,128)}, f32[1,3,1,4,32,256]{5,4,3,2,1,0:T(8,128)S(1)}, u32[]{:S(2)}) copy-start(f32[1,3,1,4,32,256]{5,4,3,2,1,0:T(8,128)S(1)} %get-tuple-element.86) | copy-start | bytes 1179652
  393.1 23.8 %copy-start.40 = (f32[1,3,1,4,32,256]{5,4,3,2,1,0:T(8,128)}, f32[1,3,1,4,32,256]{5,4,3,2,1,0:T(8,128)S(1)}, u32[]{:S(2)}) copy-start(f32[1,3,1,4,32,256]{5,4,3,2,1,0:T(8,128)S(1)} %get-tuple-element.87) | copy-start | bytes 1179652
  393.1 4.9 %copy-start.6 = (f32[1,3,2,4,32,256]{5,4,3,2,1,0:T(8,128)S(1)}, f32[1,3,2,4,32,256]{5,4,3,2,1,0:T(8,128)}, u32[]{:S(2)}) copy-start(f32[1,3,2,4,32,256]{5,4,3,2,1,0:T(8,128)} %copy-done.5) | copy-start | bytes 2359300
  395.4 5.0 %collective-permute-start.21 = (f32[1,3,2,4,1,256]{5,4,3,2,1,0:T(1,128)S(1)}, f32[1,3,2,4,1,256]{5,4,3,2,1,0:T(1,128)S(1)}, u32[]{:S(2)}, u32[]{:S(2)}) collective-permute-start(f32[1,3,2,4,1,256]{5,4,3,2,1,0:T(1,128)S(1)} %slice.2301), channel_id=1, source_target_pairs={{1,0},{3,2},{5,4},{7,6},{9,8},{11,10},{13,12},{15,14},{17,16},{19,... | collective-permute-start | bytes 73736 | tf_op jit(solution)/shard_map/ppermute | solution.py:15
  396.7 9.5 %collective-permute-start.20 = (f32[1,3,2,1,32,256]{5,4,3,2,1,0:T(8,128)S(1)}, f32[1,3,2,1,32,256]{5,4,3,2,1,0:T(8,128)S(1)}, u32[]{:S(2)}, u32[]{:S(2)}) collective-permute-start(f32[1,3,2,1,32,256]{5,4,3,2,1,0:T(8,128)S(1)} %slice.2297), channel_id=1, source_target_pairs={{2,0},{4,2},{6,4},{8,6},{10,8},{12,10},{14,12},{3,1},{5,3},{7,5},{... | collective-permute-start | bytes 589832 | tf_op jit(solution)/shard_map/ppermute | solution.py:15
  407.9 6.2 %collective-permute-start.22 = (f32[1,3,2,4,1,256]{5,4,3,2,1,0:T(1,128)S(1)}, f32[1,3,2,4,1,256]{5,4,3,2,1,0:T(1,128)S(1)}, u32[]{:S(2)}, u32[]{:S(2)}) collective-permute-start(f32[1,3,2,4,1,256]{5,4,3,2,1,0:T(1,128)S(1)} %pad_maximum_fusion.35), channel_id=1, source_target_pairs={{0,1},{2,3},{4,5},{6,7},{8,9},{10,11},{12,13},{14,15},{16,17},{18,... | collective-permute-start | bytes 73736 | tf_op jit(solution)/shard_map/ppermute | solution.py:15
  409.9 5.3 %collective-permute-start.23 = (f32[1,3,2,1,32,256]{5,4,3,2,1,0:T(8,128)S(1)}, f32[1,3,2,1,32,256]{5,4,3,2,1,0:T(8,128)S(1)}, u32[]{:S(2)}, u32[]{:S(2)}) collective-permute-start(f32[1,3,2,1,32,256]{5,4,3,2,1,0:T(8,128)S(1)} %pad_maximum_fusion.23), channel_id=1, source_target_pairs={{0,2},{2,4},{4,6},{6,8},{8,10},{10,12},{12,14},{1,3},{3,5},{5,7},{... | collective-permute-start | bytes 589832 | tf_op jit(solution)/shard_map/ppermute | solution.py:15
  419.8 3.5 copy-start.8
  464.1 4.1 copy-start.15
  464.1 4.1 copy-start.22
  464.1 4.1 copy-start.25
  464.1 4.1 copy-start.39
  464.1 4.1 copy-start.41
  468.2 1.6 copy-start.42
  468.2 1.6 copy-start.43
  468.3 1.8 copy-start.48
  468.3 2.1 copy-start.49
  468.3 2.2 copy-start.50
  468.3 2.3 copy-start.51
  (55 other events, 47.1 us)
